TPU v7x, 256 devices: a whole 4x4x8 slice. The times are simulated.
256 devices in a mesh: dp: 8 (over x, core), param: 32 (over y, z).
Axes of the slice: x: 4, y: 4, z: 8, core: 2. Of those that a mesh axis runs over, the one named last changes fastest.
Arguments:
- train_grads: bfloat16 [7168, 212992], P('dp', 'param'), as said below
- query_grads: bfloat16 [256, 212992], P('dp', 'param'), as said below
Outputs:
- scores: float32 [256, 7168], P('param', 'dp')
Inputs may be any that keep to these rules, and one draw needn't show every extreme that they name: `train_grads`: finite real values. `query_grads`: finite real values.
All inputs are finite; a program needn't handle non-finite values.
Results may differ from a plain program's by a relative error of at most 0.0003.
Values may be sent and summed in bfloat16 or wider, within the bound.
A program may use at most 64 MiB of HBM per device.

v0:
```python
import jax
import jax.numpy as jnp
from jax import lax
from jax.sharding import PartitionSpec as P

epsilon = 1e-06


def in_blocks(x, dim, devices):
    lengths = x.shape
    pieces = x.reshape(*lengths[:dim], devices, lengths[dim] // devices, *lengths[dim + 1 :])
    return jnp.moveaxis(pieces, dim, 0)


def summed_on_arrival(x, axis, dim):
    devices = lax.axis_size(axis)
    pieces = lax.all_to_all(in_blocks(x, dim, devices), axis, 0, 0, tiled=True)
    return jnp.sum(pieces, axis=0)


def side_by_side(arrays, axis, dim, along):
    columns = [a.reshape(*a.shape[:along], -1) for a in arrays]
    both = jnp.concatenate(columns, axis=along)
    out, at, done = (summed_on_arrival(both, axis, dim), 0, [])
    for a, column in zip(arrays, columns):
        slab = out[..., at : at + column.shape[along]]
        done.append(slab.reshape(*slab.shape[:along], *a.shape[along:]))
        at += column.shape[along]
    return tuple(done)


def copy_for_each(x, axis):
    devices = lax.axis_size(axis)
    return lax.all_to_all(jnp.broadcast_to(x[None], (devices, *x.shape)), axis, 0, 0, tiled=True)


def taken_together(x, axis):
    everything = copy_for_each(x, axis)
    return jnp.sum(everything, axis=0)


def per_device(train_grads, query_grads):
    queries = lax.all_gather(query_grads, "dp", axis=0, tiled=True)
    products = lax.dot_general(
        queries, train_grads, (((1,), (1,)), ((), ())), preferred_element_type=jnp.float32
    )
    query_norm = jnp.sum(jnp.square(queries.astype(jnp.float32)), axis=1)
    train_norm = jnp.sum(jnp.square(train_grads.astype(jnp.float32)), axis=1)
    products, query_norm = side_by_side((products, query_norm), "param", 0, 1)
    train_norm = taken_together(train_norm, "param")
    return (
        products
        * lax.rsqrt(query_norm + epsilon)[:, None]
        * lax.rsqrt(train_norm + epsilon)[None, :]
    )


def solution(mesh):
    return jax.shard_map(
        per_device,
        mesh=mesh,
        in_specs=(P("dp", "param"), P("dp", "param")),
        out_specs=P("param", "dp"),
        check_vma=False,
    )
```

profile of v0, /device:TPU:4, one launch (start us, length us, event | category | flops | bytes accessed | tf_op | source)
XLA Modules:
  0.0 101.4 jit_solution(12826004121880036399)
XLA Ops:
  6.5 0.0 all-gather.2.cloned.1.call-start
  6.5 0.7 all-gather.2.cloned.1.call-update
  7.3 6.8 %multiply_reduce_fusion = f32[896]{0:T(1024)S(1)} fusion(bf16[896,6656]{1,0:T(8,128)(2,1)} %param.2), kind=kLoop, calls=%fused_computation | loop fusion | flops 17890432 | bytes 11931136 | tf_op jit(solution)/shard_map/reduce_sum | solution.py:48
  14.0 0.7 broadcast_in_dim.2
  14.7 11.5 %all-to-all-start.1 = ((f32[32,1,896]{2,1,0:T(1,128)}), f32[32,1,896]{2,1,0:T(1,128)S(1)}, u32[]{:S(2)}, u32[]{:S(2)}) async-start(f32[32,1,896]{2,1,0:T(1,128)} %broadcast_in_dim.2), calls=%async_computation.1 | async-start | bytes 229376 | tf_op jit(solution)/shard_map/all_to_all | solution.py:34
  26.2 15.8 %all-gather.2.cloned.1.call-done = bf16[256,6656]{1,0:T(8,128)(2,1)} async-done(((bf16[32,6656]{1,0:T(8,128)(2,1)}), bf16[256,6656]{1,0:T(8,128)(2,1)}) %all-gather.2.cloned.1.call-update) | async-done | bytes 3407888 | tf_op jit(solution)/shard_map/all_gather | solution.py:43
  42.1 0.0 copy-start
  42.1 10.6 %convolution_bitcast_fusion = f32[32,8,896]{2,1,0:T(8,128)S(1)} fusion(bf16[256,6656]{1,0:T(8,128)(2,1)} %all-gather.2.cloned.1.call-done, bf16[896,6656]{1,0:T(8,128)(2,1)} %param.2), kind=kOutput, calls=%fused_computation.2 | convolution fusion | flops 3053453312 | bytes 16252928 | tf_op jit(solution)/shard_map/dot_general | solution.py:44
  52.7 0.0 copy-done
  52.7 0.8 multiply_reduce_fusion.1
  53.5 0.2 concatenate.11
  53.7 1.1 %pad_maximum_fusion = f32[32,8,897]{2,1,0:T(8,128)} fusion(f32[32,8,1]{2,1,0:T(8,128)S(1)} %concatenate.11, f32[32,8,896]{2,1,0:T(8,128)S(1)} %convolution_bitcast_fusion), kind=kLoop, calls=%fused_computation.3 | loop fusion | flops 229632 | bytes 1837056 | tf_op jit(solution)/shard_map/concatenate | solution.py:23
  54.8 0.0 all-to-all-done.1
  54.8 9.9 %all-to-all-start = ((f32[32,8,897]{2,1,0:T(8,128)}), f32[32,8,897]{2,1,0:T(8,128)S(1)}, u32[]{:S(2)}, u32[]{:S(2)}) async-start(f32[32,8,897]{2,1,0:T(8,128)} %pad_maximum_fusion), calls=%async_computation | async-start | bytes 2097152 | tf_op jit(solution)/shard_map/all_to_all | solution.py:17
  64.7 0.1 reduce_sum.39
  64.8 28.9 %all-to-all-done = f32[32,8,897]{2,1,0:T(8,128)S(1)} async-done(((f32[32,8,897]{2,1,0:T(8,128)}), f32[32,8,897]{2,1,0:T(8,128)S(1)}, u32[]{:S(2)}, u32[]{:S(2)}) %all-to-all-start) | async-done | bytes 918560 | tf_op jit(solution)/shard_map/all_to_all | solution.py:17
  93.7 0.1 reduce_sum.37
  93.7 0.1 fusion.2
  93.8 0.7 fusion
  (1 shorter events, 0.0 us)
Async XLA Ops:
  6.5 35.5 %all-gather.2.cloned.1.call-start = ((), (), s32[]{:S(2)}) async-start(), calls=%async_computation.2 | async-start | bytes 3833856 | tf_op jit(solution)/shard_map/all_gather | solution.py:43
  14.7 40.1 %all-to-all-start.1 = ((f32[32,1,896]{2,1,0:T(1,128)}), f32[32,1,896]{2,1,0:T(1,128)S(1)}, u32[]{:S(2)}, u32[]{:S(2)}) async-start(f32[32,1,896]{2,1,0:T(1,128)} %broadcast_in_dim.2), calls=%async_computation.1 | async-start | bytes 229376 | tf_op jit(solution)/shard_map/all_to_all | solution.py:34
  42.1 10.7 %copy-start = (bf16[256,6656]{1,0:T(8,128)(2,1)S(1)}, bf16[256,6656]{1,0:T(8,128)(2,1)}, u32[]{:S(2)}) copy-start(bf16[256,6656]{1,0:T(8,128)(2,1)} %all-gather.2.cloned.1.call-done) | copy-start | bytes 10223620
  54.8 38.9 %all-to-all-start = ((f32[32,8,897]{2,1,0:T(8,128)}), f32[32,8,897]{2,1,0:T(8,128)S(1)}, u32[]{:S(2)}, u32[]{:S(2)}) async-start(f32[32,8,897]{2,1,0:T(8,128)} %pad_maximum_fusion), calls=%async_computation | async-start | bytes 2097152 | tf_op jit(solution)/shard_map/all_to_all | solution.py:17
Sparse Core Ops, SparseCore 0:
  9.2 32.8 all-gather.1
where the time goes:
time: 103 us; the launch traced here: 101 us
  waiting for transfers between devices  45.4 us (44%)
  starting transfers between devices  21.3 us (21%)
  between operations  13.4 us (13%)
  matrix products  10.6 us (10%)
  other arithmetic  9.61 us (9%)
    all_to_all x1, waiting for transfers between devices, summed_on_arrival(): pieces = lax.all_to_all(in_blocks(x, dim, devices), axis, 0, 0, tiled=True)  28.9 us
    all_gather x1, waiting for transfers between devices, per_device(): queries = lax.all_gather(query_grads, 'dp', axis=0, tiled=True)  15.8 us
    all_to_all x1, starting transfers between devices, copy_for_each(): lax.all_to_all(jnp.broadcast_to(x[None], (devices, *x.shape)), axis, 0, 0...  11.5 us
    dot_general x1, matrix products, per_device(): lax.dot_general(queries, train_grads, (((1,), (1,)), ((), ())), preferred...  10.6 us
    all_to_all x1, starting transfers between devices, summed_on_arrival(): pieces = lax.all_to_all(in_blocks(x, dim, devices), axis, 0, 0, tiled=True)  9.85 us
    reduce_sum x1, other arithmetic, per_device(): train_norm = jnp.sum(jnp.square(train_grads.astype(jnp.float32)), axis=1)  6.77 us
  transfers between devices with their start and end apart: 3, of which 2 were waited for; matrix products, arithmetic and copies ran while one was open for 20% of the time, Pallas kernels for 0%

commit v1 on v0

v1 whole, which is shorter than its diff:
```python
import jax
import jax.numpy as jnp
from jax import lax
from jax.experimental import pallas as pl
from jax.experimental.pallas import tpu as pltpu
from jax.sharding import PartitionSpec as P

epsilon = 1e-06

NX, NY, NZ, NDP = 4, 4, 8, 8
TRAIN, DEPTH = 896, 6656
HALF = 16
LANES = 128
WIDTHS = (2048, 2048, 1536, 1024)
CUTS = tuple((sum(WIDTHS[:i]), w) for i, w in enumerate(WIDTHS))
NK = len(CUTS)
FAR_FIRST = (4, 3, 5, 2, 6, 1, 7)
GROUPS = (
    ((0, 0), (0, 1), (1, 0), (1, 1), (2, 0), (3, 0), (4, 0), (5, 0)),
    ((2, 1), (3, 1), (4, 1), (5, 1)),
    ((6, 0), (6, 1), (7, 0), (7, 1)),
)


def dot_rows(a, b):
    return lax.dot_general(a, b, (((1,), (1,)), ((), ())), preferred_element_type=jnp.float32)


def row_sums(lanes):
    high = lanes.astype(jnp.bfloat16)
    rest = lanes - high.astype(jnp.float32)
    mid = rest.astype(jnp.bfloat16)
    low = (rest - mid.astype(jnp.float32)).astype(jnp.bfloat16)
    ones = jnp.ones((16, 2 * LANES), jnp.bfloat16)
    both = jnp.concatenate([high, mid], axis=1)
    return (dot_rows(ones, both) + dot_rows(ones[:, :LANES], low))[0:1, :]


def kernel(
    train, query, out,
    q, t, p, zin, zout, zsum, yin, tacc, qall, norm, nz, nsum, ny, nall,
    q_sem, t_sem, out_sem, mate_sem, in_sem, pass_sem,
    z_send, z_recv, relay_recv, y_send, y_recv, qn_send, qn_recv, nz_send, nz_recv, ny_send, ny_recv,
):
    dp, param = lax.axis_index("dp"), lax.axis_index("param")
    x, c = dp // 2, dp % 2
    y, z = param // NZ, param % NZ
    right = (((x + 1) % NX) * 2 + c, param)
    left = (((x + NX - 1) % NX) * 2 + c, param)
    mate = (x * 2 + 1 - c, param)

    def at_z(d):
        return (dp, y * NZ + (z + d) % NZ)

    def at_y(d):
        return (dp, ((y + d) % NY) * NZ + z)

    def at_dp(d):
        return ((dp + d) % NDP, param)

    q_loads, t_loads = [], []
    for h in range(2):
        load = pltpu.make_async_copy(query.at[pl.ds(h * HALF, HALF), :], q.at[0, h], q_sem.at[h])
        load.start()
        q_loads.append(load)
    peers = [at_dp(d) for d in range(1, NDP)]
    peers += [at_z(d) for d in range(1, NZ)] + [at_y(d) for d in range(1, NY)]
    barrier = pltpu.get_barrier_semaphore()
    for peer in peers:
        pl.semaphore_signal(barrier, inc=1, device_id=peer, device_id_type=pl.DeviceIdType.MESH)

    def squares(ref_rows, k):
        total = jnp.zeros((HALF, LANES), jnp.float32)
        for j in range(CUTS[k][1] // LANES):
            v = ref_rows(pl.ds(CUTS[k][0] + j * LANES, LANES)).astype(jnp.float32)
            total = total + v * v
        return total

    for load in q_loads:
        load.wait()
    for i in range(TRAIN // LANES):
        rows = pl.ds(i * LANES, LANES)
        load = pltpu.make_async_copy(train.at[rows, :], t.at[rows, :], t_sem.at[i])
        load.start()
        t_loads.append(load)
    own = []
    for h in range(2):
        total = squares(lambda s, h=h: q[0, h, :, s], 0)
        for k in range(1, NK):
            total = total + squares(lambda s, h=h: q[0, h, :, s], k)
        own.append(total)
    own += [jnp.zeros((LANES - 2 * HALF, LANES), jnp.float32)]
    qall[dp] = row_sums(jnp.concatenate(own, axis=0))

    pl.semaphore_wait(barrier, len(peers))

    def remote(src, dst, send, recv, to):
        return pltpu.make_async_remote_copy(
            src_ref=src, dst_ref=dst, send_sem=send, recv_sem=recv, device_id=to,
            device_id_type=pl.DeviceIdType.MESH,
        )

    def await_in(like, sem):
        remote(like, like, sem, sem, mate).wait_recv()

    def await_out(like, sem):
        remote(like, like, sem, sem, mate).wait_send()

    def hop(src, dst, h, k, recv, to):
        k0, w = CUTS[k]
        piece = pl.ds(k0, w)
        remote(q.at[src, h, :, piece], q.at[dst, h, :, piece], out_sem, recv, to).start()

    for d in range(1, NDP):
        remote(qall.at[dp], qall.at[dp], qn_send, qn_recv, at_dp(d)).start()

    for h in range(2):
        for k in range(NK):
            hop(0, 2, h, k, in_sem.at[h, k], right)
            hop(0, 4, h, k, in_sem.at[h, k], left)
        remote(q.at[0, h], q.at[1, h], out_sem, mate_sem, mate).start()

    def products(g, first, last):
        k0, w = CUTS[first][0], sum(WIDTHS[first:last])
        a = jnp.concatenate([q[s, h, :, pl.ds(k0, w)] for s, h in GROUPS[g]], axis=0)
        part = dot_rows(a, t[:, pl.ds(k0, w)])
        for i, (s, h) in enumerate(GROUPS[g]):
            piece = part[i * HALF : (i + 1) * HALF].reshape(2, 8, TRAIN)
            where = pl.ds(4 * s + 2 * h, 2)
            p[where] = piece if first == 0 else p[where] + piece

    def block_of(r, zt):
        return 4 * (2 * r + (zt // 4 + c) % 2) + zt % 4

    def z_copy(src, dst, sem, d):
        remote(src, dst, z_send, sem, at_z(d)).start()

    def mine(r, d):
        return p.at[block_of(r, (z + d) % NZ)]

    def send_z(r):
        for d in FAR_FIRST:
            z_copy(mine(r, d), zin.at[r, d - 1], z_recv.at[r], d)

    PLUS, MINUS = pl.ds(0, 512), pl.ds(512, TRAIN - 512)

    def send_near(half, *groups):
        def each(d, go):
            for r in groups:
                if half is None:
                    go(r)
                else:
                    pl.when(((z + d) % NZ % 4) // 2 == half)(lambda r=r: go(r))

        def split(r):
            z_copy(mine(r, 4).at[:, PLUS], zin.at[r, 6, :, PLUS], relay_recv.at[r], 2)
            z_copy(mine(r, 4).at[:, MINUS], zin.at[r, 6, :, MINUS], relay_recv.at[r], 6)

        each(4, split)
        each(3, lambda r: z_copy(mine(r, 3), zin.at[r, 4], relay_recv.at[r], 1))
        each(5, lambda r: z_copy(mine(r, 5), zin.at[r, 5], relay_recv.at[r], 7))
        each(1, lambda r: z_copy(mine(r, 1), zin.at[r, 0], z_recv.at[r], 1))
        each(7, lambda r: z_copy(mine(r, 7), zin.at[r, 1], z_recv.at[r], 7))

    def relay(r):
        await_in(zin.at[r, pl.ds(4, 3)], relay_recv.at[r])
        for i, (d, part) in enumerate(((2, PLUS), (6, MINUS))):
            zout[r, i] = p[block_of(r, (z + d) % NZ)] + zin[r, 4 + i]
            zout[r, i, :, part] += zin[r, 6, :, part]
            z_copy(zout.at[r, i], zin.at[r, 2 + i], z_recv.at[r], d)

    home = [x, (x + NX - 1) % NX, (x + 1) % NX, (x + 2) % NX]

    def send_y(r):
        count = NZ - 1 if r == 3 else 4
        await_in(zin.at[r, pl.ds(0, count)], z_recv.at[r])
        total = p[block_of(r, z)]
        for i in range(count):
            total = total + zin[r, i]
        zsum[r] = total
        d = (home[r] + NY - y) % NY

        @pl.when(d != 0)
        def _():
            remote(zsum.at[r], yin.at[d - 1], y_send, y_recv, (dp, home[r] * NZ + z)).start()

    def arrive(g, k):
        k0, w = CUTS[k]
        await_in(q.at[2, :, :, pl.ds(k0, w)], in_sem.at[g, k])
        if g < 2:
            hop(2, 3, g, k, pass_sem.at[g, k], mate)
            hop(4, 5, g, k, pass_sem.at[g, k], mate)
            if g == 0:
                hop(2, 6, 0, k, in_sem.at[2, k], right)
            else:
                hop(4, 6, 1, k, in_sem.at[2, k], left)
        else:
            hop(6, 7, 0, k, pass_sem.at[2, k], mate)
            hop(6, 7, 1, k, pass_sem.at[2, k], mate)

    def multiply(g, first, last):
        if g == 0 and first == 0:
            await_in(q.at[1], mate_sem)
        for k in range(first, last):
            k0, w = CUTS[k]
            await_in(q.at[2, :, :, pl.ds(k0, w)], pass_sem.at[g, k])

        @pl.when(x >= 0)
        def _():
            products(g, first, last)

    def train_norms(first, last):
        def rows_of(i, carry):
            rows = pl.ds(pl.multiple_of(i * HALF, HALF), HALF)
            total = squares(lambda s: t[rows, s], 0)
            for k in range(1, NK):
                total = total + squares(lambda s, k=k: t[rows, s], k)
            tacc[rows, :] = total
            return carry

        for i in range(first, last):
            t_loads[i].wait()
            lax.fori_loop(i * LANES // HALF, (i + 1) * LANES // HALF, rows_of, 0)

    def send_norms():
        row = row_sums(tacc[...])
        await_in(qall.at[pl.ds(0, NDP - 1)], qn_recv)
        for i in range(NDP):
            norm[pl.ds(i, 1), :] = qall[i]
        for i in range(TRAIN // LANES):
            norm[pl.ds(NDP + i, 1), :] = row[:, i * LANES : (i + 1) * LANES]
        norm[pl.ds(15, 1), :] = jnp.zeros((1, LANES), jnp.float32)
        for d in FAR_FIRST:
            remote(norm, nz.at[d - 1], nz_send, nz_recv, at_z(d)).start()

    def add_norms():
        await_in(nz, nz_recv)
        total = norm[...]
        for d in range(NZ - 1):
            total = total + nz[d]
        nsum[...] = total
        for d in range(1, NY):
            remote(nsum, ny.at[d - 1], ny_send, ny_recv, at_y(d)).start()

    todo = [
        (train_norms, 0, 5),
        (arrive, 0, 0),
        (train_norms, 5, 7),
        (arrive, 0, 1),
        (arrive, 0, 2),
        (send_norms,),
        (arrive, 0, 3),
        (multiply, 0, 0, 2),
        (arrive, 1, 0),
        (arrive, 1, 1),
        (multiply, 0, 2, 4),
        (send_near, None, 0),
        (send_near, 0, 1, 2),
        (arrive, 1, 2),
        (arrive, 1, 3),
        (multiply, 1, 0, 2),
        (arrive, 2, 0),
        (multiply, 1, 2, 4),
        (relay, 0),
        (send_near, 1, 1, 2),
        (add_norms,),
        (arrive, 2, 1),
        (multiply, 2, 0, 1),
        (arrive, 2, 2),
        (multiply, 2, 1, 2),
        (arrive, 2, 3),
        (multiply, 2, 2, 3),
        (relay, 1),
        (relay, 2),
        (multiply, 2, 3, 4),
        (send_z, 3),
        (send_y, 0),
        (send_y, 1),
        (send_y, 2),
        (send_y, 3),
    ]
    for what, *how in todo:
        what(*how)

    await_in(ny, ny_recv)
    norms = nsum[...]
    for d in range(NY - 1):
        norms = norms + ny[d]
    nall[...] = norms
    train_norm = jnp.concatenate([norms[NDP + i : NDP + i + 1, :] for i in range(TRAIN // LANES)], axis=1)
    lane = lax.broadcasted_iota(jnp.int32, (8, LANES), 1)
    sub = lax.broadcasted_iota(jnp.int32, (8, LANES), 0)
    rows_norm = jnp.broadcast_to(nall[pl.ds(2 * y + z // 4, 1), :], (8, LANES))
    query_norm = jnp.sum(jnp.where(lane == sub + 8 * (z % 4), rows_norm, 0.0), axis=1, keepdims=True)
    query_scale = lax.rsqrt(query_norm + epsilon)
    train_scale = lax.rsqrt(train_norm + epsilon)

    ahead = (y + NX - x) % NX
    total = zsum[jnp.where(ahead == 0, 0, jnp.where(ahead == 3, 1, ahead + 1))]
    await_in(yin, y_recv)
    for d in range(NY - 1):
        total = total + yin[d]
    out[...] = total * query_scale * train_scale

    await_out(q.at[pl.ds(0, 7)], out_sem)
    await_out(zin, z_send)
    await_out(yin, y_send)
    await_out(qall.at[pl.ds(0, NDP - 1)], qn_send)
    await_out(nz, nz_send)
    await_out(ny, ny_send)


def per_device(train_grads, query_grads):
    f32, bf16 = jnp.float32, jnp.bfloat16
    dma = pltpu.SemaphoreType.DMA
    return pl.pallas_call(
        kernel,
        name="scores",
        out_shape=jax.ShapeDtypeStruct((8, TRAIN), f32),
        in_specs=[pl.BlockSpec(memory_space=pl.ANY)] * 2,
        out_specs=pl.BlockSpec(memory_space=pltpu.VMEM),
        scratch_shapes=[
            pltpu.VMEM((8, 2, HALF, DEPTH), bf16),
            pltpu.VMEM((TRAIN, DEPTH), bf16),
            pltpu.VMEM((32, 8, TRAIN), f32),
            pltpu.VMEM((4, NZ - 1, 8, TRAIN), f32),
            pltpu.VMEM((3, 2, 8, TRAIN), f32),
            pltpu.VMEM((4, 8, TRAIN), f32),
            pltpu.VMEM((NY - 1, 8, TRAIN), f32),
            pltpu.VMEM((TRAIN, LANES), f32),
            pltpu.VMEM((NDP, 1, LANES), f32),
            pltpu.VMEM((16, LANES), f32),
            pltpu.VMEM((NZ - 1, 16, LANES), f32),
            pltpu.VMEM((16, LANES), f32),
            pltpu.VMEM((NY - 1, 16, LANES), f32),
            pltpu.VMEM((16, LANES), f32),
            dma((2,)),
            dma((TRAIN // LANES,)),
            dma(()),
            dma(()),
            dma((3, NK)),
            dma((3, NK)),
            dma(()),
            dma((4,)),
            dma((3,)),
        ]
        + [dma(())] * 8,
        compiler_params=pltpu.CompilerParams(
            collective_id=0, has_side_effects=True, vmem_limit_bytes=66_700_000
        ),
    )(train_grads, query_grads)


def solution(mesh):
    return jax.shard_map(
        per_device,
        mesh=mesh,
        in_specs=(P("dp", "param"), P("dp", "param")),
        out_specs=P("param", "dp"),
        check_vma=False,
    )
```

time: 103 us -> 44.8 us (0.43); the launches traced: 101 us -> 44.6 us
  waiting for transfers between devices: 45.4 us -> 0 us
  Pallas kernels: 0 us -> 43.3 us
  starting transfers between devices: 21.3 us -> 0 us
  between operations: 13.4 us -> 0.01 us
  matrix products: 10.6 us -> 0 us
  other arithmetic: 9.61 us -> 0 us
    pallas_call x0 -> x1, Pallas kernels: none -> 43.3 us  [per_device(): pl.pallas_call(kernel, name='scores', out_shape=jax.ShapeDtypeStruct((8,...]
    all_to_all x2 -> x0, waiting for transfers between devices: 28.9 us -> none  [the longest x1 28.9 us: summed_on_arrival(): pieces = lax.all_to_all(in_blocks(x, dim, devices), axis, 0, 0, tiled=True)]
    all_to_all x2 -> x0, starting transfers between devices: 21.3 us -> none  [the longest x1 11.5 us: copy_for_each(): lax.all_to_all(jnp.broadcast_to(x[None], (devices, *x.shape)), axis, 0, 0...]
    all_gather x1 -> x0, waiting for transfers between devices: 15.8 us -> none  [per_device(): queries = lax.all_gather(query_grads, 'dp', axis=0, tiled=True)]
    dot_general x1 -> x0, matrix products: 10.6 us -> none  [per_device(): lax.dot_general(queries, train_grads, (((1,), (1,)), ((), ())), preferred...]
    reduce_sum x4 -> x0, other arithmetic: 7.68 us -> none  [the longest x1 6.77 us: per_device(): train_norm = jnp.sum(jnp.square(train_grads.astype(jnp.float32)), axis=1)]
    unnamed x2 -> x1, local copies, waits for them, and re-layouts: 0.01 us -> 1.36 us
    concatenate x1 -> x0, other arithmetic: 1.11 us -> none  [side_by_side(): both = jnp.concatenate(columns, axis=along)]
  transfers between devices with their start and end apart: 3 -> 0, of which waited for: 2 -> 0; matrix products, arithmetic and copies ran while one was open for 20% -> 0% of each run, Pallas kernels for 0% -> 0%
where the time goes in v1:
time: 44.8 us; the launch traced here: 44.6 us
  Pallas kernels  43.3 us (97%)
  local copies, waits for them, and re-layouts  1.36 us (3%)
    pallas_call x1, Pallas kernels, per_device(): pl.pallas_call(kernel, name='scores', out_shape=jax.ShapeDtypeStruct((8,...  43.3 us
    unnamed x1, local copies, waits for them, and re-layouts  1.36 us

profile of v1, /device:TPU:4, one launch (start us, length us, event | category | flops | bytes accessed | tf_op | source)
XLA Modules:
  0.0 44.6 jit_solution(2679565105089078396)
XLA Ops:
  0.0 43.3 %scores.1 = f32[8,896]{1,0:T(8,128)} custom-call(bf16[896,6656]{1,0:T(8,128)(2,1)} %train.1, bf16[32,6656]{1,0:T(8,128)(2,1)} %query.1), custom_call_target="tpu_custom_call" | custom-call | tf_op jit(solution)/shard_map/scores/pallas_call | solution.py:316
  43.3 1.4 %copy.4 = f32[8,896]{1,0:T(8,128)} copy(f32[8,896]{1,0:T(8,128)} %scores.1) | data formatting | bytes 57344

commit v2 on v1

--- a/solution.py
+++ b/solution.py
@@ -16,8 +16,8 @@
 NK = len(CUTS)
 FAR_FIRST = (4, 3, 5, 2, 6, 1, 7)
 GROUPS = (
-    ((0, 0), (0, 1), (1, 0), (1, 1), (2, 0), (3, 0), (4, 0), (5, 0)),
-    ((2, 1), (3, 1), (4, 1), (5, 1)),
+    ((0, 0), (0, 1), (1, 0), (1, 1)),
+    tuple((s, h) for s in range(2, 6) for h in range(2)),
     ((6, 0), (6, 1), (7, 0), (7, 1)),
 )
 
@@ -39,7 +39,7 @@
 def kernel(
     train, query, out,
     q, t, p, zin, zout, zsum, yin, tacc, qall, norm, nz, nsum, ny, nall,
-    q_sem, t_sem, out_sem, mate_sem, in_sem, pass_sem,
+    far_sem, q_sem, t_sem, out_sem, mate_sem, in_sem, pass_sem,
     z_send, z_recv, relay_recv, y_send, y_recv, qn_send, qn_recv, nz_send, nz_recv, ny_send, ny_recv,
 ):
     dp, param = lax.axis_index("dp"), lax.axis_index("param")
@@ -63,8 +63,7 @@
         load = pltpu.make_async_copy(query.at[pl.ds(h * HALF, HALF), :], q.at[0, h], q_sem.at[h])
         load.start()
         q_loads.append(load)
-    peers = [at_dp(d) for d in range(1, NDP)]
-    peers += [at_z(d) for d in range(1, NZ)] + [at_y(d) for d in range(1, NY)]
+    peers = [right, left, mate, at_z(1), at_z(NZ - 1), at_y(1), at_y(NY - 1)]
     barrier = pltpu.get_barrier_semaphore()
     for peer in peers:
         pl.semaphore_signal(barrier, inc=1, device_id=peer, device_id_type=pl.DeviceIdType.MESH)
@@ -111,14 +110,35 @@
         piece = pl.ds(k0, w)
         remote(q.at[src, h, :, piece], q.at[dst, h, :, piece], out_sem, recv, to).start()
 
-    for d in range(1, NDP):
-        remote(qall.at[dp], qall.at[dp], qn_send, qn_recv, at_dp(d)).start()
-
+    def tell(*steps):
+        for i, whom in steps:
+            for peer in whom:
+                pl.semaphore_signal(far_sem.at[i], inc=1, device_id=peer, device_id_type=pl.DeviceIdType.MESH)
+
+    def told(*steps):
+        for i, whom in steps:
+            pl.semaphore_wait(far_sem.at[i], len(whom))
+
+    around = (right, left, mate)
+    along_z, along_y = peers[3:5], peers[5:7]
+    tell((0, around), (1, along_z), (2, along_y))
     for h in range(2):
         for k in range(NK):
             hop(0, 2, h, k, in_sem.at[h, k], right)
             hop(0, 4, h, k, in_sem.at[h, k], left)
         remote(q.at[0, h], q.at[1, h], out_sem, mate_sem, mate).start()
+
+    def meet(step):
+        if step == 0:
+            told((0, around), (1, along_z), (2, along_y))
+            tell((3, around), (4, along_z))
+        elif step == 1:
+            told((3, around), (4, along_z))
+            tell((5, along_z))
+        else:
+            told((5, along_z))
+            for d in range(1, NDP):
+                remote(qall.at[dp], qall.at[dp], qn_send, qn_recv, at_dp(d)).start()
 
     def products(g, first, last):
         k0, w = CUTS[first][0], sum(WIDTHS[first:last])
@@ -138,29 +158,17 @@
     def mine(r, d):
         return p.at[block_of(r, (z + d) % NZ)]
 
-    def send_z(r):
-        for d in FAR_FIRST:
-            z_copy(mine(r, d), zin.at[r, d - 1], z_recv.at[r], d)
-
     PLUS, MINUS = pl.ds(0, 512), pl.ds(512, TRAIN - 512)
 
-    def send_near(half, *groups):
-        def each(d, go):
-            for r in groups:
-                if half is None:
-                    go(r)
-                else:
-                    pl.when(((z + d) % NZ % 4) // 2 == half)(lambda r=r: go(r))
-
-        def split(r):
+    def send_z(*groups):
+        for r in groups:
             z_copy(mine(r, 4).at[:, PLUS], zin.at[r, 6, :, PLUS], relay_recv.at[r], 2)
             z_copy(mine(r, 4).at[:, MINUS], zin.at[r, 6, :, MINUS], relay_recv.at[r], 6)
-
-        each(4, split)
-        each(3, lambda r: z_copy(mine(r, 3), zin.at[r, 4], relay_recv.at[r], 1))
-        each(5, lambda r: z_copy(mine(r, 5), zin.at[r, 5], relay_recv.at[r], 7))
-        each(1, lambda r: z_copy(mine(r, 1), zin.at[r, 0], z_recv.at[r], 1))
-        each(7, lambda r: z_copy(mine(r, 7), zin.at[r, 1], z_recv.at[r], 7))
+            z_copy(mine(r, 3), zin.at[r, 4], relay_recv.at[r], 1)
+            z_copy(mine(r, 5), zin.at[r, 5], relay_recv.at[r], 7)
+        for r in groups:
+            z_copy(mine(r, 1), zin.at[r, 0], z_recv.at[r], 1)
+            z_copy(mine(r, 7), zin.at[r, 1], z_recv.at[r], 7)
 
     def relay(r):
         await_in(zin.at[r, pl.ds(4, 3)], relay_recv.at[r])
@@ -172,10 +180,9 @@
     home = [x, (x + NX - 1) % NX, (x + 1) % NX, (x + 2) % NX]
 
     def send_y(r):
-        count = NZ - 1 if r == 3 else 4
-        await_in(zin.at[r, pl.ds(0, count)], z_recv.at[r])
+        await_in(zin.at[r, pl.ds(0, 4)], z_recv.at[r])
         total = p[block_of(r, z)]
-        for i in range(count):
+        for i in range(4):
             total = total + zin[r, i]
         zsum[r] = total
         d = (home[r] + NY - y) % NY
@@ -203,7 +210,8 @@
             await_in(q.at[1], mate_sem)
         for k in range(first, last):
             k0, w = CUTS[k]
-            await_in(q.at[2, :, :, pl.ds(k0, w)], pass_sem.at[g, k])
+            for part in ((), (0, 1), (2,))[g]:
+                await_in(q.at[2, :, :, pl.ds(k0, w)], pass_sem.at[part, k])
 
         @pl.when(x >= 0)
         def _():
@@ -244,37 +252,40 @@
 
     todo = [
         (train_norms, 0, 5),
+        (meet, 0),
+        (train_norms, 5, TRAIN // LANES),
+        (meet, 1),
+        (multiply, 0, 0, 2),
+        (meet, 2),
         (arrive, 0, 0),
-        (train_norms, 5, 7),
         (arrive, 0, 1),
+        (multiply, 0, 2, 4),
+        (send_z, 0),
         (arrive, 0, 2),
-        (send_norms,),
         (arrive, 0, 3),
-        (multiply, 0, 0, 2),
         (arrive, 1, 0),
         (arrive, 1, 1),
-        (multiply, 0, 2, 4),
-        (send_near, None, 0),
-        (send_near, 0, 1, 2),
+        (multiply, 1, 0, 1),
         (arrive, 1, 2),
         (arrive, 1, 3),
-        (multiply, 1, 0, 2),
+        (multiply, 1, 1, 2),
+        (relay, 0),
+        (send_norms,),
         (arrive, 2, 0),
         (multiply, 1, 2, 4),
-        (relay, 0),
-        (send_near, 1, 1, 2),
+        (send_z, 1, 2),
+        (arrive, 2, 1),
+        (arrive, 2, 2),
+        (multiply, 2, 0, 1),
         (add_norms,),
-        (arrive, 2, 1),
-        (multiply, 2, 0, 1),
-        (arrive, 2, 2),
-        (multiply, 2, 1, 2),
         (arrive, 2, 3),
-        (multiply, 2, 2, 3),
-        (relay, 1),
-        (relay, 2),
+        (multiply, 2, 1, 3),
         (multiply, 2, 3, 4),
         (send_z, 3),
         (send_y, 0),
+        (relay, 1),
+        (relay, 2),
+        (relay, 3),
         (send_y, 1),
         (send_y, 2),
         (send_y, 3),
@@ -324,7 +335,7 @@
             pltpu.VMEM((TRAIN, DEPTH), bf16),
             pltpu.VMEM((32, 8, TRAIN), f32),
             pltpu.VMEM((4, NZ - 1, 8, TRAIN), f32),
-            pltpu.VMEM((3, 2, 8, TRAIN), f32),
+            pltpu.VMEM((4, 2, 8, TRAIN), f32),
             pltpu.VMEM((4, 8, TRAIN), f32),
             pltpu.VMEM((NY - 1, 8, TRAIN), f32),
             pltpu.VMEM((TRAIN, LANES), f32),
@@ -334,6 +345,7 @@
             pltpu.VMEM((16, LANES), f32),
             pltpu.VMEM((NY - 1, 16, LANES), f32),
             pltpu.VMEM((16, LANES), f32),
+            pltpu.SemaphoreType.REGULAR((6,)),
             dma((2,)),
             dma((TRAIN // LANES,)),
             dma(()),
@@ -342,7 +354,7 @@
             dma((3, NK)),
             dma(()),
             dma((4,)),
-            dma((3,)),
+            dma((4,)),
         ]
         + [dma(())] * 8,
         compiler_params=pltpu.CompilerParams(

time: 44.8 us -> 43.3 us (0.967)
  Pallas kernels: 43.3 us -> 41.6 us
    pallas_call x1, Pallas kernels: 43.3 us -> 41.6 us  [per_device(): pl.pallas_call(kernel, name='scores', out_shape=jax.ShapeDtypeStruct((8,...]
where the time goes in v2:
time: 43.3 us; the launch traced here: 42.9 us
  Pallas kernels  41.6 us (96%)
  local copies, waits for them, and re-layouts  1.36 us (3%)
    pallas_call x1, Pallas kernels, per_device(): pl.pallas_call(kernel, name='scores', out_shape=jax.ShapeDtypeStruct((8,...  41.6 us
    unnamed x1, local copies, waits for them, and re-layouts  1.36 us

profile of v2, /device:TPU:4, one launch (start us, length us, event | category | flops | bytes accessed | tf_op | source)
XLA Modules:
  0.0 42.9 jit_solution(10429246435821963790)
XLA Ops:
  0.0 41.6 %scores.1 = f32[8,896]{1,0:T(8,128)} custom-call(bf16[896,6656]{1,0:T(8,128)(2,1)} %train.1, bf16[32,6656]{1,0:T(8,128)(2,1)} %query.1), custom_call_target="tpu_custom_call" | custom-call | tf_op jit(solution)/shard_map/scores/pallas_call | solution.py:327
  41.6 1.4 %copy.4 = f32[8,896]{1,0:T(8,128)} copy(f32[8,896]{1,0:T(8,128)} %scores.1) | data formatting | bytes 57344

commit v3 on v2

--- a/solution.py
+++ b/solution.py
@@ -230,14 +230,16 @@
             t_loads[i].wait()
             lax.fori_loop(i * LANES // HALF, (i + 1) * LANES // HALF, rows_of, 0)
 
+    def fill_norms():
+        row = row_sums(tacc[...])
+        for i in range(TRAIN // LANES):
+            norm[pl.ds(NDP + i, 1), :] = row[:, i * LANES : (i + 1) * LANES]
+        norm[pl.ds(15, 1), :] = jnp.zeros((1, LANES), jnp.float32)
+
     def send_norms():
-        row = row_sums(tacc[...])
         await_in(qall.at[pl.ds(0, NDP - 1)], qn_recv)
         for i in range(NDP):
             norm[pl.ds(i, 1), :] = qall[i]
-        for i in range(TRAIN // LANES):
-            norm[pl.ds(NDP + i, 1), :] = row[:, i * LANES : (i + 1) * LANES]
-        norm[pl.ds(15, 1), :] = jnp.zeros((1, LANES), jnp.float32)
         for d in FAR_FIRST:
             remote(norm, nz.at[d - 1], nz_send, nz_recv, at_z(d)).start()
 
@@ -254,6 +256,7 @@
         (train_norms, 0, 5),
         (meet, 0),
         (train_norms, 5, TRAIN // LANES),
+        (fill_norms,),
         (meet, 1),
         (multiply, 0, 0, 2),
         (meet, 2),
@@ -277,7 +280,6 @@
         (arrive, 2, 1),
         (arrive, 2, 2),
         (multiply, 2, 0, 1),
-        (add_norms,),
         (arrive, 2, 3),
         (multiply, 2, 1, 3),
         (multiply, 2, 3, 4),
@@ -286,6 +288,7 @@
         (relay, 1),
         (relay, 2),
         (relay, 3),
+        (add_norms,),
         (send_y, 1),
         (send_y, 2),
         (send_y, 3),

time: 43.3 us -> 41.4 us (0.956); the launches traced: 42.9 us -> 40.6 us
  Pallas kernels: 41.6 us -> 39.2 us
    pallas_call x1, Pallas kernels: 41.6 us -> 39.2 us  [per_device(): pl.pallas_call(kernel, name='scores', out_shape=jax.ShapeDtypeStruct((8,...]
where the time goes in v3:
time: 41.4 us; the launch traced here: 40.6 us
  Pallas kernels  39.2 us (95%)
  local copies, waits for them, and re-layouts  1.36 us (3%)
    pallas_call x1, Pallas kernels, per_device(): pl.pallas_call(kernel, name='scores', out_shape=jax.ShapeDtypeStruct((8,...  39.2 us
    unnamed x1, local copies, waits for them, and re-layouts  1.36 us

profile of v3, /device:TPU:4, one launch (start us, length us, event | category | flops | bytes accessed | tf_op | source)
XLA Modules:
  0.0 40.6 jit_solution(3846414209791091695)
XLA Ops:
  0.0 39.2 %scores.1 = f32[8,896]{1,0:T(8,128)} custom-call(bf16[896,6656]{1,0:T(8,128)(2,1)} %train.1, bf16[32,6656]{1,0:T(8,128)(2,1)} %query.1), custom_call_target="tpu_custom_call" | custom-call | tf_op jit(solution)/shard_map/scores/pallas_call | solution.py:330
  39.2 1.4 %copy.4 = f32[8,896]{1,0:T(8,128)} copy(f32[8,896]{1,0:T(8,128)} %scores.1) | data formatting | bytes 57344

commit v4 on v3

--- a/solution.py
+++ b/solution.py
@@ -122,10 +122,11 @@
     around = (right, left, mate)
     along_z, along_y = peers[3:5], peers[5:7]
     tell((0, around), (1, along_z), (2, along_y))
+    for k in range(NK):
+        for h in range(2):
+            hop(0, 2, h, k, in_sem.at[0, k], right)
+            hop(0, 4, h, k, in_sem.at[0, k], left)
     for h in range(2):
-        for k in range(NK):
-            hop(0, 2, h, k, in_sem.at[h, k], right)
-            hop(0, 4, h, k, in_sem.at[h, k], left)
         remote(q.at[0, h], q.at[1, h], out_sem, mate_sem, mate).start()
 
     def meet(step):
@@ -191,27 +192,27 @@
         def _():
             remote(zsum.at[r], yin.at[d - 1], y_send, y_recv, (dp, home[r] * NZ + z)).start()
 
+    def pieces(g, k):
+        return q.at[pl.ds(2, 2) if g == 1 else 2, :, :, pl.ds(*CUTS[k])]
+
     def arrive(g, k):
-        k0, w = CUTS[k]
-        await_in(q.at[2, :, :, pl.ds(k0, w)], in_sem.at[g, k])
-        if g < 2:
-            hop(2, 3, g, k, pass_sem.at[g, k], mate)
-            hop(4, 5, g, k, pass_sem.at[g, k], mate)
-            if g == 0:
-                hop(2, 6, 0, k, in_sem.at[2, k], right)
+        await_in(pieces(g, k), in_sem.at[g - 1, k])
+        for h in range(2):
+            if g == 1:
+                hop(2, 3, h, k, pass_sem.at[0, k], mate)
+                hop(4, 5, h, k, pass_sem.at[0, k], mate)
             else:
-                hop(4, 6, 1, k, in_sem.at[2, k], left)
-        else:
-            hop(6, 7, 0, k, pass_sem.at[2, k], mate)
-            hop(6, 7, 1, k, pass_sem.at[2, k], mate)
+                hop(6, 7, h, k, pass_sem.at[1, k], mate)
+        if g == 1:
+            hop(2, 6, 0, k, in_sem.at[1, k], right)
+            hop(4, 6, 1, k, in_sem.at[1, k], left)
 
     def multiply(g, first, last):
         if g == 0 and first == 0:
             await_in(q.at[1], mate_sem)
-        for k in range(first, last):
-            k0, w = CUTS[k]
-            for part in ((), (0, 1), (2,))[g]:
-                await_in(q.at[2, :, :, pl.ds(k0, w)], pass_sem.at[part, k])
+        if g > 0:
+            for k in range(first, last):
+                await_in(pieces(g, k), pass_sem.at[g - 1, k])
 
         @pl.when(x >= 0)
         def _():
@@ -260,28 +261,26 @@
         (meet, 1),
         (multiply, 0, 0, 2),
         (meet, 2),
-        (arrive, 0, 0),
-        (arrive, 0, 1),
+        (arrive, 1, 0),
         (multiply, 0, 2, 4),
         (send_z, 0),
-        (arrive, 0, 2),
-        (arrive, 0, 3),
-        (arrive, 1, 0),
         (arrive, 1, 1),
         (multiply, 1, 0, 1),
         (arrive, 1, 2),
-        (arrive, 1, 3),
         (multiply, 1, 1, 2),
         (relay, 0),
         (send_norms,),
+        (arrive, 1, 3),
+        (multiply, 1, 2, 3),
         (arrive, 2, 0),
-        (multiply, 1, 2, 4),
+        (multiply, 1, 3, 4),
         (send_z, 1, 2),
         (arrive, 2, 1),
+        (multiply, 2, 0, 1),
         (arrive, 2, 2),
-        (multiply, 2, 0, 1),
+        (multiply, 2, 1, 2),
         (arrive, 2, 3),
-        (multiply, 2, 1, 3),
+        (multiply, 2, 2, 3),
         (multiply, 2, 3, 4),
         (send_z, 3),
         (send_y, 0),
@@ -353,8 +352,8 @@
             dma((TRAIN // LANES,)),
             dma(()),
             dma(()),
-            dma((3, NK)),
-            dma((3, NK)),
+            dma((2, NK)),
+            dma((2, NK)),
             dma(()),
             dma((4,)),
             dma((4,)),

time: 41.4 us -> 40.9 us (0.988); the launches traced: 40.6 us -> 40.6 us
  no operation moved by 1% of the time
where the time goes in v4:
time: 40.9 us; the launch traced here: 40.6 us
  Pallas kernels  39.2 us (96%)
  local copies, waits for them, and re-layouts  1.36 us (3%)
    pallas_call x1, Pallas kernels, per_device(): pl.pallas_call(kernel, name='scores', out_shape=jax.ShapeDtypeStruct((8,...  39.2 us
    unnamed x1, local copies, waits for them, and re-layouts  1.36 us

profile of v4, /device:TPU:4, one launch (start us, length us, event | category | flops | bytes accessed | tf_op | source)
XLA Modules:
  0.0 40.6 jit_solution(4484409106535088951)
XLA Ops:
  0.0 39.2 %scores.1 = f32[8,896]{1,0:T(8,128)} custom-call(bf16[896,6656]{1,0:T(8,128)(2,1)} %train.1, bf16[32,6656]{1,0:T(8,128)(2,1)} %query.1), custom_call_target="tpu_custom_call" | custom-call | tf_op jit(solution)/shard_map/scores/pallas_call | solution.py:329
  39.2 1.4 %copy.4 = f32[8,896]{1,0:T(8,128)} copy(f32[8,896]{1,0:T(8,128)} %scores.1) | data formatting | bytes 57344

commit v5 on v4

--- a/solution.py
+++ b/solution.py
@@ -269,10 +269,10 @@
         (arrive, 1, 2),
         (multiply, 1, 1, 2),
         (relay, 0),
-        (send_norms,),
         (arrive, 1, 3),
         (multiply, 1, 2, 3),
         (arrive, 2, 0),
+        (send_norms,),
         (multiply, 1, 3, 4),
         (send_z, 1, 2),
         (arrive, 2, 1),

time: 40.9 us -> 40.9 us (level)
  no operation moved by 1% of the time
where the time goes in v5:
time: 40.9 us; the launch traced here: 40.6 us
  Pallas kernels  39.2 us (96%)
  local copies, waits for them, and re-layouts  1.36 us (3%)
    pallas_call x1, Pallas kernels, per_device(): pl.pallas_call(kernel, name='scores', out_shape=jax.ShapeDtypeStruct((8,...  39.2 us
    unnamed x1, local copies, waits for them, and re-layouts  1.36 us

profile of v5, /device:TPU:4, one launch (start us, length us, event | category | flops | bytes accessed | tf_op | source)
XLA Modules:
  0.0 40.6 jit_solution(11757922704311594200)
XLA Ops:
  0.0 39.2 %scores.1 = f32[8,896]{1,0:T(8,128)} custom-call(bf16[896,6656]{1,0:T(8,128)(2,1)} %train.1, bf16[32,6656]{1,0:T(8,128)(2,1)} %query.1), custom_call_target="tpu_custom_call" | custom-call | tf_op jit(solution)/shard_map/scores/pallas_call | solution.py:329
  39.2 1.4 %copy.4 = f32[8,896]{1,0:T(8,128)} copy(f32[8,896]{1,0:T(8,128)} %scores.1) | data formatting | bytes 57344
